TPU v7x, 32 devices: a whole 2x2x4 slice. The times are simulated.
32 devices in a mesh: dp: 4 (over y, x), mp: 8 (over z, core).
Axes of the slice: x: 2, y: 2, z: 4, core: 2. Of those that a mesh axis runs over, the one named last changes fastest.
Arguments:
- block_input: bfloat16 [2048, 8, 2048], P('mp', 'dp'), may hold values from -6 to 6
- segments: int32 [8, 2048], P('dp'), may hold values from 0 to 5, never falling along the last dimension, each value on 1 to 1024 neighbouring positions
- key_keep: int32 [8, 2048], P('dp'), may hold values 0 or 1
- ln1_gain: float32 [2048], replicated, may hold values from 0.5 to 1.5
- ln1_bias: float32 [2048], replicated, may hold values from -1 to 1
- w_query: bfloat16 [2048, 2048], P(None, 'mp'), may hold values from -0.125 to 0.125
- b_query: float32 [2048], P('mp'), may hold values from -2.5 to 2.5
- w_keyval: bfloat16 [2048, 256], replicated, may hold values from -0.125 to 0.125
- b_value: float32 [128], replicated, may hold values from -2.5 to 2.5
- w_out: bfloat16 [2048, 2048], P('mp'), may hold values from -1 to 1
- b_out: float32 [2048], replicated, may hold values from -1.5 to 1.5
- ln2_gain: float32 [2048], replicated, may hold values from 0.5 to 1.5
- ln2_bias: float32 [2048], replicated, may hold values from -1 to 1
- w_up: bfloat16 [2048, 8192], P(None, 'mp'), may hold values from -0.125 to 0.125
- b_up: float32 [8192], P('mp'), may hold values from -2.5 to 2.5
- w_down: bfloat16 [8192, 2048], P('mp'), may hold values from -0.0625 to 0.0625
- b_down: float32 [2048], replicated, may hold values from -1.5 to 1.5
- cotangent: bfloat16 [2048, 8, 2048], P('mp', 'dp'), may hold values from -6 to 6
Outputs:
- result: bfloat16 [2048, 8, 2048], P('mp', 'dp')
- grad_input: bfloat16 [2048, 8, 2048], P('mp', 'dp')
- grad_ln1_gain: float32 [2048], replicated
- grad_ln1_bias: float32 [2048], replicated
- grad_w_query: float32 [2048, 2048], P(None, 'mp')
- grad_b_query: float32 [2048], P('mp')
- grad_w_keyval: float32 [2048, 256], replicated
- grad_b_value: float32 [128], replicated
- grad_w_out: float32 [2048, 2048], P('mp')
- grad_b_out: float32 [2048], replicated
- grad_ln2_gain: float32 [2048], replicated
- grad_ln2_bias: float32 [2048], replicated
- grad_w_up: float32 [2048, 8192], P(None, 'mp')
- grad_b_up: float32 [8192], P('mp')
- grad_w_down: float32 [8192, 2048], P('mp')
- grad_b_down: float32 [2048], replicated
Inputs may be any that keep to these rules, and one draw needn't show every extreme that they name: `segments`: along each row the document numbers never fall; each of the 6 documents of a row holds one to half of 2048 positions. `key_keep`: a position always attends itself whatever its mark.
All inputs are finite; a program needn't handle non-finite values. No bound on the sum of `key_keep` on one device may be relied on, other than what follows from the above.
Results may differ from a plain program's by a relative error of at most 0.017.
Values may be sent and summed in bfloat16 or wider, within the bound.
A program may use at most 320 MiB of HBM per device.

v0:
```python
import jax
import jax.numpy as jnp
from jax import lax
from jax.sharding import PartitionSpec as P

HD = 128


EPS = 1e-05
NEG = -1000000000.0


def layer_norm(values, norm_gain, norm_shift):
    average = jnp.mean(values, axis=-1, keepdims=True)
    centred = values - average
    variance = jnp.mean(centred * centred, axis=-1, keepdims=True)
    return centred * lax.rsqrt(variance + EPS) * norm_gain + norm_shift


def block_allowed(segments, key_keep, offset, blocks):
    length = segments.shape[1]
    positions = jnp.arange(length, dtype=jnp.int32)
    places = offset + jnp.arange(blocks, dtype=jnp.int32)
    segment_block = lax.dynamic_slice_in_dim(segments, offset, blocks, 1)
    earlier = positions[None, None, :] <= places[None, :, None]
    same_doc = segments[:, None, :] == segment_block[:, :, None]
    open_key = (key_keep[:, None, :] == 1) | (positions[None, None, :] == places[None, :, None])
    return earlier & same_doc & open_key


def block_scores(query_block, keys_all, allowed):
    scores = jnp.einsum(
        "qrhe,kre->rhqk", query_block, keys_all, preferred_element_type=jnp.float32
    ) * HD ** (-0.5)
    return jnp.where(allowed[:, None], scores, NEG)


def attention_forward(queries, keys_all, values_all, segments, key_keep):
    length, row_count, heads = (queries.shape[0], queries.shape[1], queries.shape[2])
    blocks = min(512, length)
    block_count = length // blocks

    def one_block(element):
        query_block, offset = element
        scores = block_scores(
            query_block, keys_all, block_allowed(segments, key_keep, offset, blocks)
        )
        highest = jnp.max(scores, axis=-1, keepdims=True)
        exponent = jnp.exp(scores - highest)
        totals = jnp.sum(exponent, axis=-1, keepdims=True)
        weights = (exponent / totals).astype(jnp.bfloat16)
        attended = jnp.einsum(
            "rhqk,kre->qrhe", weights, values_all, preferred_element_type=jnp.float32
        ).astype(jnp.bfloat16)
        return (attended, (highest + jnp.log(totals))[..., 0])

    offsets = jnp.arange(block_count, dtype=jnp.int32) * blocks
    attended, log_totals = lax.map(
        one_block, (queries.reshape(block_count, blocks, row_count, heads, HD), offsets)
    )
    return (attended.reshape(length, row_count, heads * HD), log_totals)


def attention_backward(
    queries, keys_all, values_all, segments, key_keep, log_totals, grad_attended
):
    length, row_count, heads = (queries.shape[0], queries.shape[1], queries.shape[2])
    blocks = min(512, length)
    block_count = length // blocks
    scale = HD ** (-0.5)

    def one_block(carry, element):
        grad_keys, grad_values = carry
        query_block, grad_block, log_block, offset = element
        allowed = block_allowed(segments, key_keep, offset, blocks)
        scores = block_scores(query_block, keys_all, allowed)
        probability = jnp.where(allowed[:, None], jnp.exp(scores - log_block[..., None]), 0.0)
        grad_prob = jnp.einsum(
            "qrhe,kre->rhqk", grad_block, values_all, preferred_element_type=jnp.float32
        )
        grad_scores = (
            probability * (grad_prob - jnp.sum(grad_prob * probability, axis=-1, keepdims=True))
        ).astype(jnp.bfloat16)
        grad_query = (
            jnp.einsum("rhqk,kre->qrhe", grad_scores, keys_all, preferred_element_type=jnp.float32)
            * scale
        ).astype(jnp.bfloat16)
        grad_keys = (
            grad_keys
            + jnp.einsum(
                "rhqk,qrhe->kre", grad_scores, query_block, preferred_element_type=jnp.float32
            )
            * scale
        )
        grad_values = grad_values + jnp.einsum(
            "rhqk,qrhe->kre",
            probability.astype(jnp.bfloat16),
            grad_block,
            preferred_element_type=jnp.float32,
        )
        return ((grad_keys, grad_values), grad_query)

    offsets = jnp.arange(block_count, dtype=jnp.int32) * blocks
    empty = jnp.zeros((length, row_count, HD), jnp.float32)
    shaped = (
        queries.reshape(block_count, blocks, row_count, heads, HD),
        grad_attended.reshape(block_count, blocks, row_count, heads, HD),
        log_totals,
        offsets,
    )
    (grad_keys, grad_values), grad_queries = lax.scan(one_block, (empty, empty), shaped)
    return (grad_queries.reshape(length, row_count, heads * HD), grad_keys, grad_values)


def body(
    block_input,
    segments,
    key_keep,
    ln1_gain,
    ln1_bias,
    w_query,
    b_query,
    w_keyval,
    b_value,
    w_out,
    b_out,
    ln2_gain,
    ln2_bias,
    w_up,
    b_up,
    w_down,
    b_down,
    cotangent,
):
    heads = w_query.shape[1] // HD
    local_input = block_input.astype(jnp.float32)

    def project(normed_full):
        queries = (
            jnp.einsum("lrd,dc->lrc", normed_full, w_query, preferred_element_type=jnp.float32)
            + b_query
        ).astype(jnp.bfloat16)
        projected = jnp.einsum(
            "lrd,dc->lrc", normed_full, w_keyval, preferred_element_type=jnp.float32
        )
        keys_all = projected[..., :HD].astype(jnp.bfloat16)
        values_all = (projected[..., HD:] + b_value).astype(jnp.bfloat16)
        return (
            queries.reshape(queries.shape[0], queries.shape[1], heads, HD),
            keys_all,
            values_all,
        )

    def expand(normed_two_full):
        return (
            jnp.einsum("lrd,df->lrf", normed_two_full, w_up, preferred_element_type=jnp.float32)
            + b_up
        )

    normed_local = layer_norm(local_input, ln1_gain, ln1_bias).astype(jnp.bfloat16)
    normed_full = lax.all_gather(normed_local, "mp", axis=0, tiled=True)
    queries, keys_all, values_all = project(normed_full)
    attended, log_totals = attention_forward(queries, keys_all, values_all, segments, key_keep)
    piece = attended
    mixed_sum = lax.psum_scatter(
        jnp.einsum("lrc,cd->lrd", piece, w_out, preferred_element_type=jnp.float32),
        "mp",
        scatter_dimension=0,
        tiled=True,
    )
    residual = local_input + mixed_sum + b_out
    normed_two_local = layer_norm(residual, ln2_gain, ln2_bias).astype(jnp.bfloat16)
    normed_two_full = lax.all_gather(normed_two_local, "mp", axis=0, tiled=True)
    pre_act = expand(normed_two_full)
    activated = jax.nn.gelu(pre_act, approximate=True).astype(jnp.bfloat16)
    piece = activated
    grown = lax.psum_scatter(
        jnp.einsum("lrf,fd->lrd", piece, w_down, preferred_element_type=jnp.float32).astype(
            jnp.bfloat16
        ),
        "mp",
        scatter_dimension=0,
        tiled=True,
    ).astype(jnp.float32)
    result = (residual + grown + b_down).astype(jnp.bfloat16)
    grad_full = lax.all_gather(cotangent, "mp", axis=0, tiled=True)
    grad_w_down = jnp.einsum(
        "lrf,lrd->fd", activated, grad_full, preferred_element_type=jnp.float32
    )
    grad_act = jnp.einsum("lrd,fd->lrf", grad_full, w_down, preferred_element_type=jnp.float32)
    normed_two_full = lax.all_gather(normed_two_local, "mp", axis=0, tiled=True)
    pre_act = expand(normed_two_full)
    gelu_value, gelu_pull = jax.vjp(lambda inner: jax.nn.gelu(inner, approximate=True), pre_act)
    grad_pre = gelu_pull(grad_act)[0].astype(jnp.bfloat16)
    grad_b_up = jnp.sum(grad_pre, axis=(0, 1), dtype=jnp.float32)
    grad_w_up = jnp.einsum(
        "lrd,lrf->df", normed_two_full, grad_pre, preferred_element_type=jnp.float32
    )
    piece = grad_pre
    grad_normed_two = lax.psum_scatter(
        jnp.einsum("lrf,df->lrd", piece, w_up, preferred_element_type=jnp.float32),
        "mp",
        scatter_dimension=0,
        tiled=True,
    )
    norm_two_value, norm_two_pull = jax.vjp(layer_norm, residual, ln2_gain, ln2_bias)
    grad_resid_part, grad_ln2_gain, grad_ln2_bias = norm_two_pull(grad_normed_two)
    grad_residual = cotangent.astype(jnp.float32) + grad_resid_part
    grad_b_out = jnp.sum(grad_residual, axis=(0, 1))
    grad_b_down = jnp.sum(cotangent, axis=(0, 1), dtype=jnp.float32)
    grad_mixed_local = grad_residual.astype(jnp.bfloat16)
    grad_mixed = lax.all_gather(grad_mixed_local, "mp", axis=0, tiled=True)
    grad_w_out = jnp.einsum("lrc,lrd->cd", attended, grad_mixed, preferred_element_type=jnp.float32)
    grad_attended = jnp.einsum(
        "lrd,cd->lrc", grad_mixed, w_out, preferred_element_type=jnp.float32
    ).astype(jnp.bfloat16)
    normed_full = lax.all_gather(normed_local, "mp", axis=0, tiled=True)
    queries, keys_all, values_all = project(normed_full)
    grad_queries, grad_keys, grad_values = attention_backward(
        queries, keys_all, values_all, segments, key_keep, log_totals, grad_attended
    )
    grad_keyval = lax.psum_scatter(
        jnp.concatenate([grad_keys, grad_values], axis=-1).astype(jnp.bfloat16),
        "mp",
        scatter_dimension=0,
        tiled=True,
    )
    grad_b_query = jnp.sum(grad_queries, axis=(0, 1), dtype=jnp.float32)
    grad_w_query = jnp.einsum(
        "lrd,lrc->dc", normed_full, grad_queries, preferred_element_type=jnp.float32
    )
    piece = grad_queries
    grad_normed = lax.psum_scatter(
        jnp.einsum("lrc,dc->lrd", piece, w_query, preferred_element_type=jnp.float32).astype(
            jnp.bfloat16
        ),
        "mp",
        scatter_dimension=0,
        tiled=True,
    ).astype(jnp.float32)
    grad_normed = grad_normed + jnp.einsum(
        "lrk,dk->lrd", grad_keyval, w_keyval, preferred_element_type=jnp.float32
    )
    grad_w_keyval = jnp.einsum(
        "lrd,lrk->dk", normed_local, grad_keyval, preferred_element_type=jnp.float32
    )
    grad_b_value = jnp.sum(grad_keyval[..., HD:], axis=(0, 1), dtype=jnp.float32)
    norm_one_value, norm_one_pull = jax.vjp(layer_norm, local_input, ln1_gain, ln1_bias)
    grad_local, grad_ln1_gain, grad_ln1_bias = norm_one_pull(grad_normed)
    grad_input = (grad_residual + grad_local).astype(jnp.bfloat16)
    shared = lax.psum(
        (
            grad_w_keyval,
            grad_b_value,
            grad_ln1_gain,
            grad_ln1_bias,
            grad_ln2_gain,
            grad_ln2_bias,
            grad_b_out,
            grad_b_down,
        ),
        ("dp", "mp"),
    )
    sharded = (
        lax.psum(grad_w_query.astype(jnp.bfloat16), "dp").astype(jnp.float32),
        lax.psum(grad_b_query.astype(jnp.bfloat16), "dp").astype(jnp.float32),
        lax.psum(grad_w_out.astype(jnp.bfloat16), "dp").astype(jnp.float32),
        lax.psum(grad_w_up.astype(jnp.bfloat16), "dp").astype(jnp.float32),
        lax.psum(grad_b_up.astype(jnp.bfloat16), "dp").astype(jnp.float32),
        lax.psum(grad_w_down.astype(jnp.bfloat16), "dp").astype(jnp.float32),
    )
    return (
        result,
        grad_input,
        shared[2],
        shared[3],
        sharded[0],
        sharded[1],
        shared[0],
        shared[1],
        sharded[2],
        shared[6],
        shared[4],
        shared[5],
        sharded[3],
        sharded[4],
        sharded[5],
        shared[7],
    )


def solution(mesh):
    return jax.shard_map(
        body,
        mesh=mesh,
        in_specs=(
            P("mp", "dp", None),
            P("dp", None),
            P("dp", None),
            P(),
            P(),
            P(None, "mp"),
            P("mp"),
            P(),
            P(),
            P("mp", None),
            P(),
            P(),
            P(),
            P(None, "mp"),
            P("mp"),
            P("mp", None),
            P(),
            P("mp", "dp", None),
        ),
        out_specs=(
            P("mp", "dp", None),
            P("mp", "dp", None),
            P(),
            P(),
            P(None, "mp"),
            P("mp"),
            P(),
            P(),
            P("mp", None),
            P(),
            P(),
            P(),
            P(None, "mp"),
            P("mp"),
            P("mp", None),
            P(),
        ),
        check_vma=False,
    )
```

profile of v0, /device:TPU:0, one launch (start us, length us, event | category | flops | bytes accessed | tf_op | source)
XLA Modules:
  0.0 2518.6 jit_solution(13815937075262068085)
XLA Ops:
  16.8 153.9 %all-gather.5.cloned.1.call-done = bf16[2048,2,2048]{2,0,1:T(8,128)(2,1)} async-done(((bf16[256,2,2048]{2,0,1:T(8,128)(2,1)}), bf16[2048,2,2048]{2,0,1:T(8,128)(2,1)}) %all-gather.5.cloned.1.call-update) | async-done | bytes 16777232 | tf_op jit(solution)/shard_map/all_gather | solution.py:161
  196.2 101.0 %while.27 = (s32[]{:T(128)}, bf16[4,512,2,2,128]{4,3,1,0,2:T(2,128)(2,1)}, f32[4,2,2,512]{3,2,1,0:T(2,128)}, s32[4]{0:T(128)S(1)}, s32[2,2048]{1,0:T(2,128)S(1)}...) while((s32[]{:T(128)}, ...), condition=%wide.region_5.6_spmd, body=%wide.region_2.5_spmd.sunk | while | flops 2208565760 | bytes 67231928 | solution.py:58
  302.0 15.1 fusion.74
  317.2 323.8 %reduce-scatter.6.cloned.1.call-done = f32[256,2,2048]{2,0,1:T(8,128)} async-done(((f32[2048,2,2048]{2,0,1:T(8,128)}), f32[256,2,2048]{2,0,1:T(8,128)}) %reduce-scatter.6.cloned.1.call-update) | async-done | bytes 4194320 | tf_op jit(solution)/shard_map/reduce_scatter | solution.py:165
  651.7 147.3 %all-gather.7.cloned.1.call-done = bf16[2048,2,2048]{2,0,1:T(8,128)(2,1)} async-done(((bf16[256,2,2048]{2,0,1:T(8,128)(2,1)}), bf16[2048,2,2048]{2,0,1:T(8,128)(2,1)}) %all-gather.7.cloned.1.call-update) | async-done | bytes 16777232 | tf_op jit(solution)/shard_map/all_gather | solution.py:173
  799.0 23.4 fusion.65
  822.5 127.9 %all-gather.9.cloned.1.call-done = bf16[2048,2,2048]{2,0,1:T(8,128)(2,1)} async-done(((bf16[256,2,2048]{2,0,1:T(8,128)(2,1)}), bf16[2048,2,2048]{2,0,1:T(8,128)(2,1)}) %all-gather.9.cloned.1.call-update) | async-done | bytes 16777232 | tf_op jit(solution)/shard_map/all_gather | solution.py:186
  950.4 36.7 %fusion.87 = (bf16[1024]{0:T(1024)(128)(2,1)}, bf16[2048,2,1024]{2,0,1:T(8,128)(2,1)}) fusion(f32[2048,2,1024]{2,0,1:T(8,128)} %fusion.65, f32[1024]{0:T(1024)S(1)} %copy-done.63, bf16[2048,2,2048]{2,0,1:T(8,128)(2,1)} %all-gather.9.cloned.1.call-done, bf16[1024,2048]{1,0:T(8,128)(2,1)} %param.37), kind=kOutput, calls=%fused_computation.147 | convolution fusion | flops 17272143872 | bytes 46143488 | tf_op jit(solution)/shard_map/lrd,fd->lrf/dot_general | solution.py:190
  987.0 24.5 fusion.63
  1011.6 26.5 %convolution_convert_fusion.1 = bf16[2048,2,2048]{2,0,1:T(8,128)(2,1)} fusion(bf16[1024,2048]{1,0:T(8,128)(2,1)} %param.37, f32[2048,2,1024]{2,0,1:T(8,128)} %fusion.65, f32[1024]{0:T(1024)S(1)} %copy-done.63), kind=kOutput, calls=%fused_computation.75 | convolution fusion | flops 17230200832 | bytes 37752832 | tf_op jit(solution)/shard_map/lrf,fd->lrd/dot_general | solution.py:178
  1038.2 297.1 %reduce-scatter.10.cloned.1.call-done = f32[256,2,2048]{2,0,1:T(8,128)} async-done(((f32[2048,2,2048]{2,0,1:T(8,128)}), f32[256,2,2048]{2,0,1:T(8,128)}) %reduce-scatter.10.cloned.1.call-update) | async-done | bytes 4194320 | tf_op jit(solution)/shard_map/reduce_scatter | solution.py:200
  1340.6 163.6 %reduce-scatter.8.cloned.1.call-done = bf16[256,2,2048]{2,0,1:T(8,128)(2,1)} async-done(((bf16[2048,2,2048]{2,0,1:T(8,128)(2,1)}), bf16[256,2,2048]{2,0,1:T(8,128)(2,1)}) %reduce-scatter.8.cloned.1.call-update) | async-done | bytes 2097168 | tf_op jit(solution)/shard_map/reduce_scatter | solution.py:177
  1513.7 23.7 bitcast_convert_fusion.1
  1537.4 125.9 %all-gather.11.cloned.1.call-done = bf16[2048,2,2048]{2,0,1:T(8,128)(2,1)} async-done(((bf16[256,2,2048]{2,0,1:T(8,128)(2,1)}), bf16[2048,2,2048]{2,0,1:T(8,128)(2,1)}) %all-gather.11.cloned.1.call-update) | async-done | bytes 16777232 | tf_op jit(solution)/shard_map/all_gather | solution.py:212
  1677.1 259.4 %while.28 = (s32[]{:T(128)}, f32[2048,2,128]{0,2,1:T(8,128)S(1)}, f32[2048,2,128]{0,2,1:T(8,128)}, bf16[4,512,2,2,128]{4,1,3,2,0:T(8,128)(2,1)}, bf16[4,512,2,2,...) while((s32[]{:T(128)}, f32[2048,2,128]{0,2,1:T(8,128)S(1)}, ...), condition=%wide.region_15.16_spmd.clone, body=%wide.region_13.15_spmd.clone.sunk | while | flops 5424286208 | bytes 277447072 | solution.py:111
  1695.8 15.3 fusion.133
  1760.5 15.4 fusion.133
  1825.2 15.4 fusion.133
  1889.9 15.4 fusion.133
  1939.9 27.3 %bitcast_convert_fusion = bf16[1024,2048]{1,0:T(8,128)(2,1)} fusion(bf16[2048,2,2048]{2,0,1:T(8,128)(2,1)} %all-gather.9.cloned.1.call-done, f32[2048,2,1024]{2,0,1:T(8,128)} %fusion.65, f32[1024]{0:T(1024)S(1)} %copy-done.64), kind=kOutput, calls=%fused_computation.76 | convolution fusion | flops 17223909376 | bytes 37752832 | tf_op jit(solution)/shard_map/lrf,lrd->fd/dot_general | solution.py:187
  2027.0 171.9 %all-reduce.8.cloned.1.call-done = (bf16[2048,256]{1,0:T(8,128)(2,1)}, bf16[256,2048]{1,0:T(8,128)(2,1)}, bf16[2048,1024]{1,0:T(8,128)(2,1)}, bf16[1024,2048]{1,0:T(8,128)(2,1)}) async-done(((bf16[2048,256]{1,0:T(8,128)(2,1)}, bf16[256,2048]{1,0:T(8,128)(2,1)}, bf16[2048,1024]{1,0:T(8,128)(2,1)}, bf16[1024,2048]{1,0:T(8,128)(2,1)}), (bf16[2048,256]{1,0:T(8,128)(2,1)}, bf16[256,2048]{1,0:T(8,128)(2,1)}, ...) | async-done | bytes 10485776 | tf_op jit(solution)/shard_map/psum | solution.py:265
  2213.8 155.8 %reduce-scatter.12.cloned.1.call-done = bf16[256,2,2048]{2,0,1:T(8,128)(2,1)} async-done(((bf16[2048,2,2048]{2,0,1:T(8,128)(2,1)}), bf16[256,2,2048]{2,0,1:T(8,128)(2,1)}) %reduce-scatter.12.cloned.1.call-update) | async-done | bytes 2097168 | tf_op jit(solution)/shard_map/reduce_scatter | solution.py:233
  2382.9 39.4 %all-reduce = (f32[2048]{0:T(1024)}, f32[2048]{0:T(1024)}, f32[128]{0:T(128)}, f32[2048]{0:T(1024)}, f32[2048]{0:T(1024)}, /*index=5*/f32[2048]{0:T(1024)}, f32[2048]{0:T(1024)}) all-reduce(f32[2048]{0:T(1024)S(1)} %get-tuple-element.248, f32[2048]{0:T(1024)S(1)} %get-tuple-element.251, ...), channel_id=1, replica_groups=mesh['dp'=4,'mp'=8] {'dp','mp'}, use_global_device_ids=true, to_apply=%region_21.22 | all-reduce | flops 12416 | bytes 99328 | tf_op jit(solution)/shard_map/psum | solution.py:251
  2422.2 86.7 %all-reduce.6.cloned.1.call-done = f32[2048,256]{1,0:T(8,128)} async-done(((f32[2048,256]{1,0:T(8,128)}), f32[2048,256]{1,0:T(8,128)}) %all-reduce.6.cloned.1.call-update) | async-done | bytes 2097168 | tf_op jit(solution)/shard_map/psum | solution.py:251
  (348 shorter events, 455.6 us)
Async XLA Ops:
  7.2 294.8 %copy-start = (bf16[256,2048]{1,0:T(8,128)(2,1)S(1)}, bf16[256,2048]{1,0:T(8,128)(2,1)}, u32[]{:S(2)}) copy-start(bf16[256,2048]{1,0:T(8,128)(2,1)} %param.31) | copy-start | bytes 3145732
  7.2 163.4 %all-gather.5.cloned.1.call-start = ((), (), s32[]{:S(2)}) async-start(), calls=%async_computation.5 | async-start | bytes 18874368 | tf_op jit(solution)/shard_map/all_gather | solution.py:161
  10.2 160.5 %copy-start.65 = (f32[256]{0:T(256)S(1)}, f32[256]{0:T(256)}, u32[]{:S(2)}) copy-start(f32[256]{0:T(256)} %param.28) | copy-start | bytes 3076
  16.7 624.2 %reduce-scatter.6.cloned.1.call-start = ((), (), s32[]{:S(2)}) async-start(), calls=%async_computation.6 | async-start | bytes 37748736 | tf_op jit(solution)/shard_map/reduce_scatter | solution.py:165
  317.1 323.9 %copy-start.9 = (bf16[256,2,2048]{2,1,0:T(2,128)(2,1)S(1)}, bf16[256,2,2048]{2,1,0:T(2,128)(2,1)}, u32[]{:S(2)}) copy-start(bf16[256,2,2048]{2,1,0:T(2,128)(2,1)} %param.22) | copy-start | bytes 6291460
  317.1 323.9 %copy-start.56 = (f32[2048]{0:T(1024)S(1)}, f32[2048]{0:T(1024)}, u32[]{:S(2)}) copy-start(f32[2048]{0:T(1024)} %param.32) | copy-start | bytes 24580
  317.1 481.9 %all-gather.7.cloned.1.call-start = ((), (), s32[]{:S(2)}) async-start(), calls=%async_computation.7 | async-start | bytes 18874368 | tf_op jit(solution)/shard_map/all_gather | solution.py:173
  649.3 301.0 %all-gather.9.cloned.1.call-start = ((), (), s32[]{:S(2)}) async-start(), calls=%async_computation.9 | async-start | bytes 18874368 | tf_op jit(solution)/shard_map/all_gather | solution.py:186
  651.6 298.7 %copy-start.63 = (f32[1024]{0:T(1024)S(1)}, f32[1024]{0:T(1024)}, u32[]{:S(2)}) copy-start(f32[1024]{0:T(1024)} %param.36) | copy-start | bytes 12292
  651.6 683.7 %reduce-scatter.10.cloned.1.call-start = ((), (), s32[]{:S(2)}) async-start(), calls=%async_computation.10 | async-start | bytes 37748736 | tf_op jit(solution)/shard_map/reduce_scatter | solution.py:200
  1011.5 492.7 %reduce-scatter.8.cloned.1.call-start = ((), (), s32[]{:S(2)}) async-start(), calls=%async_computation.8 | async-start | bytes 18874368 | tf_op jit(solution)/shard_map/reduce_scatter | solution.py:177
  1038.1 297.2 %copy-start.34 = (f32[2048]{0:T(1024)S(1)}, f32[2048]{0:T(1024)}, u32[]{:S(2)}) copy-start(f32[2048]{0:T(1024)} %param.33) | copy-start | bytes 24580
  1038.1 297.2 %copy-start.38 = (f32[256,2]{0,1:T(2,128)S(1)}, f32[256,2]{0,1:T(2,128)}, u32[]{:S(2)}) copy-start(f32[256,2]{0,1:T(2,128)} %copy-done.37) | copy-start | bytes 6148
  1038.1 297.2 %copy-start.44 = (f32[256,2]{0,1:T(2,128)S(1)}, f32[256,2]{0,1:T(2,128)}, u32[]{:S(2)}) copy-start(f32[256,2]{0,1:T(2,128)} %copy-done.43) | copy-start | bytes 6148
  1038.1 302.4 %copy-start.50 = (f32[256,2]{0,1:T(2,128)S(1)}, f32[256,2]{0,1:T(2,128)}, u32[]{:S(2)}) copy-start(f32[256,2]{0,1:T(2,128)} %copy-done.49) | copy-start | bytes 6148
  1038.1 466.0 %copy-start.58 = (f32[2048]{0:T(1024)S(1)}, f32[2048]{0:T(1024)}, u32[]{:S(2)}) copy-start(f32[2048]{0:T(1024)} %param.38) | copy-start | bytes 24580
  1038.1 625.2 %all-gather.11.cloned.1.call-start = ((), (), s32[]{:S(2)}) async-start(), calls=%async_computation.11 | async-start | bytes 18874368 | tf_op jit(solution)/shard_map/all_gather | solution.py:212
  1340.6 169.4 %copy-start.18 = (bf16[256,2,2048]{2,1,0:T(2,128)(2,1)S(1)}, bf16[256,2,2048]{2,1,0:T(2,128)(2,1)}, u32[]{:S(2)}) copy-start(bf16[256,2,2048]{2,1,0:T(2,128)(2,1)} %param.39) | copy-start | bytes 6291460
  1513.7 510.1 %reduce-scatter.14.cloned.1.call-start = ((), (), s32[]{:S(2)}) async-start(), calls=%async_computation.13 | async-start | bytes 2359296 | tf_op jit(solution)/shard_map/reduce_scatter | solution.py:222
  1939.8 259.1 %all-reduce.8.cloned.1.call-start = ((), (), s32[]{:S(2)}) async-start(), calls=%async_computation.15 | async-start | bytes 20971520 | tf_op jit(solution)/shard_map/psum | solution.py:265
  1994.1 375.6 %reduce-scatter.12.cloned.1.call-start = ((), (), s32[]{:S(2)}) async-start(), calls=%async_computation.12 | async-start | bytes 18874368 | tf_op jit(solution)/shard_map/reduce_scatter | solution.py:233
  2004.3 504.6 %all-reduce.6.cloned.1.call-start = ((), (), s32[]{:S(2)}) async-start(), calls=%async_computation.14 | async-start | bytes 4194304 | tf_op jit(solution)/shard_map/psum | solution.py:251
  2209.4 160.2 %copy-start.36 = (f32[2048]{0:T(1024)S(1)}, f32[2048]{0:T(1024)}, u32[]{:S(2)}) copy-start(f32[2048]{0:T(1024)} %param.25) | copy-start | bytes 24580
  2209.4 160.2 %copy-start.40 = (f32[256,2]{0,1:T(2,128)S(1)}, f32[256,2]{0,1:T(2,128)}, u32[]{:S(2)}) copy-start(f32[256,2]{0,1:T(2,128)} %copy-done.39) | copy-start | bytes 6148
  (73 other events, 1155.4 us)
Sparse Core Ops, SparseCore 0:
  16.8 153.7 all-gather.4
  317.3 323.6 reduce-scatter.5
  649.5 149.5 all-gather.6
  801.1 149.2 all-gather.8
  1011.6 323.6 reduce-scatter.9
  1337.5 166.5 reduce-scatter.7
  1513.8 149.5 all-gather.10
  1939.9 34.2 reduce-scatter.13
  1994.2 204.6 all-reduce.7
  2201.1 168.4 reduce-scatter.11
  2375.5 133.3 all-reduce.5
where the time goes:
time: 2530 us; the launch traced here: 2520 us
  waiting for transfers between devices  1750 us (69%)
  matrix products  423 us (17%)
  other arithmetic  179 us (7%)
  local copies, waits for them, and re-layouts  81 us (3%)
  blocking collectives  50.3 us (2%)
    reduce_scatter x1, waiting for transfers between devices, body(): lax.psum_scatter(jnp.einsum('lrc,cd->lrd', piece, w_out, preferred_elemen...  324 us
    reduce_scatter x1, waiting for transfers between devices, body(): lax.psum_scatter(jnp.einsum('lrf,df->lrd', piece, w_up, preferred_element...  297 us
    psum x1, waiting for transfers between devices, body(): lax.psum(grad_w_query.astype(jnp.bfloat16), 'dp').astype(jnp.float32)  172 us
    reduce_scatter x1, waiting for transfers between devices, body(): lax.psum_scatter(jnp.einsum('lrf,fd->lrd', piece, w_down, preferred_eleme...  164 us
    reduce_scatter x1, waiting for transfers between devices, body(): lax.psum_scatter(jnp.einsum('lrc,dc->lrd', piece, w_query, preferred_elem...  156 us
    all_gather x1, waiting for transfers between devices, body(): normed_full = lax.all_gather(normed_local, 'mp', axis=0, tiled=True)  154 us
    all_gather x1, waiting for transfers between devices, body(): normed_two_full = lax.all_gather(normed_two_local, 'mp', axis=0, tiled=True)  147 us
    all_gather x1, waiting for transfers between devices, body(): grad_full = lax.all_gather(cotangent, 'mp', axis=0, tiled=True)  128 us
  transfers between devices with their start and end apart: 11, of which 10 were waited for; matrix products, arithmetic and copies ran while one was open for 7% of the time, Pallas kernels for 0%

commit v1 on v0

v1 whole, which is shorter than its diff:
```python
import functools
import math

import jax
import jax.numpy as jnp
from jax import lax
from jax.experimental import pallas as pl
from jax.experimental.pallas import tpu as pltpu
from jax.sharding import PartitionSpec as P

HD = 128
EPS = 1e-05
NEG = -1000000000.0
LOG2E = math.log2(math.e)
BF = jnp.bfloat16
F32 = jnp.float32
GROUP = 4


def layer_norm(values, norm_gain, norm_shift):
    average = jnp.mean(values, axis=-1, keepdims=True)
    centred = values - average
    variance = jnp.mean(centred * centred, axis=-1, keepdims=True)
    return centred * lax.rsqrt(variance + EPS) * norm_gain + norm_shift


def dot(left, right, dims=((1,), (0,))):
    return lax.dot_general(left, right, (dims, ((), ())), preferred_element_type=F32)


def forward_kernel(span, q_ref, kv_ref, bias_ref, o_ref, log_ref, vt, acc, top, total):
    row = pl.program_id(0)
    first, mine = span[row], span[pl.num_programs(0)]
    heads = q_ref.shape[1] // HD
    factor = HD ** (-0.5) * LOG2E

    @pl.loop(first, mine + 1)
    def _(j):
        vt[j] = kv_ref[j, 0, :, HD:].T

    for start in range(0, heads, GROUP):
        group = range(start, min(start + GROUP, heads))

        def block(j, initial):
            keys = kv_ref[j, 0, :, :HD]
            mask = bias_ref[j, 0].astype(F32)
            for g, head in enumerate(group):
                query = q_ref[:, head * HD : (head + 1) * HD]
                score = dot(keys, query, ((1,), (1,))) * factor + mask
                high = jnp.max(score, axis=0, keepdims=True)
                if not initial:
                    old = top[g]
                    high = jnp.maximum(high, old)
                    fade = jnp.exp2(old - high)
                part = jnp.exp2(score - high)
                size = jnp.sum(part, axis=0, keepdims=True)
                mixed = dot(vt[j], part.astype(BF))
                top[g] = high
                total[g] = size if initial else total[g] * fade + size
                acc[g] = mixed if initial else acc[g] * fade + mixed

        block(mine, True)

        @pl.loop(first, mine)
        def _(j):
            block(j, False)

        for g, head in enumerate(group):
            size = total[g]
            o_ref[:, head * HD : (head + 1) * HD] = (acc[g] / size).T.astype(BF)
            log_ref[0, head : head + 1, :] = top[g] + jnp.log2(size)


def attention_forward(span, queries, keyval, bias, rows):
    tokens, width = queries.shape
    length = tokens // rows
    blocks = keyval.shape[0]
    heads = width // HD
    return pl.pallas_call(
        forward_kernel,
        out_shape=(
            jax.ShapeDtypeStruct((tokens, width), BF),
            jax.ShapeDtypeStruct((rows, heads, length), F32),
        ),
        grid_spec=pltpu.PrefetchScalarGridSpec(
            num_scalar_prefetch=1,
            grid=(rows,),
            in_specs=[
                pl.BlockSpec((length, width), lambda r, s: (r, 0)),
                pl.BlockSpec((blocks, 1, length, 2 * HD), lambda r, s: (0, r, 0, 0)),
                pl.BlockSpec((blocks, 1, length, length), lambda r, s: (0, r, 0, 0)),
            ],
            out_specs=(
                pl.BlockSpec((length, width), lambda r, s: (r, 0)),
                pl.BlockSpec((1, heads, length), lambda r, s: (r, 0, 0)),
            ),
            scratch_shapes=[
                pltpu.VMEM((blocks, HD, length), BF),
                pltpu.VMEM((GROUP, HD, length), F32),
                pltpu.VMEM((GROUP, 1, length), F32),
                pltpu.VMEM((GROUP, 1, length), F32),
            ],
        ),
        compiler_params=pltpu.CompilerParams(vmem_limit_bytes=40 * 2**20),
        cost_estimate=pl.CostEstimate(
            flops=rows * heads * length * 4 * length * HD * 4,
            bytes_accessed=4 * tokens * width,
            transcendentals=rows * heads * length * 4 * length,
        ),
        name="attention_forward",
    )(span, queries, keyval, bias)


def backward_kernel(
    span, q_ref, do_ref, o_ref, kv_ref, bias_ref, log_ref, dq_ref, dkv_ref,
    kt, dk, dv, dqt, delta,
):
    row = pl.program_id(0)
    first, mine = span[row], span[pl.num_programs(0)]
    heads = q_ref.shape[1] // HD
    scale = HD ** (-0.5)
    factor = scale * LOG2E

    dkv_ref[...] = jnp.zeros_like(dkv_ref)

    @pl.loop(first, mine + 1)
    def _(j):
        kt[j] = kv_ref[j, 0, :, :HD].T
        dk[j] = jnp.zeros(dk.shape[1:], F32)
        dv[j] = jnp.zeros(dv.shape[1:], F32)

    for head in range(heads):
        cols = slice(head * HD, (head + 1) * HD)
        product = do_ref[:, cols].astype(F32) * o_ref[:, cols].astype(F32)
        delta[head] = jnp.sum(product.T, axis=0, keepdims=True)

    for start in range(0, heads, GROUP):
        group = range(start, min(start + GROUP, heads))

        def block(j, initial):
            keys = kv_ref[j, 0, :, :HD]
            values = kv_ref[j, 0, :, HD:]
            mask = bias_ref[j, 0].astype(F32)
            sum_k, sum_v = dk[j], dv[j]
            for g, head in enumerate(group):
                query = q_ref[:, head * HD : (head + 1) * HD]
                grad = do_ref[:, head * HD : (head + 1) * HD]
                score = dot(keys, query, ((1,), (1,))) * factor + mask
                prob = jnp.exp2(score - log_ref[0, head : head + 1, :])
                grad_prob = dot(values, grad, ((1,), (1,)))
                grad_score = (prob * (grad_prob - delta[head])).astype(BF)
                sum_v = sum_v + dot(prob.astype(BF), grad)
                sum_k = sum_k + dot(grad_score, query)
                part = dot(kt[j], grad_score)
                dqt[g] = part if initial else dqt[g] + part
            dk[j] = sum_k
            dv[j] = sum_v

        block(mine, True)

        @pl.loop(first, mine)
        def _(j):
            block(j, False)

        for g, head in enumerate(group):
            dq_ref[:, head * HD : (head + 1) * HD] = (dqt[g] * scale).T.astype(BF)

    @pl.loop(first, mine + 1)
    def _(j):
        dkv_ref[j, 0, :, :HD] = (dk[j] * scale).astype(BF)
        dkv_ref[j, 0, :, HD:] = dv[j].astype(BF)


def attention_backward(span, queries, grad_out, out, keyval, bias, logs, rows):
    tokens, width = queries.shape
    length = tokens // rows
    blocks = keyval.shape[0]
    heads = width // HD
    slab = pl.BlockSpec((length, width), lambda r, s: (r, 0))
    pairs = pl.BlockSpec((blocks, 1, length, 2 * HD), lambda r, s: (0, r, 0, 0))
    return pl.pallas_call(
        backward_kernel,
        out_shape=(
            jax.ShapeDtypeStruct((tokens, width), BF),
            jax.ShapeDtypeStruct(keyval.shape, BF),
        ),
        grid_spec=pltpu.PrefetchScalarGridSpec(
            num_scalar_prefetch=1,
            grid=(rows,),
            in_specs=[
                slab,
                slab,
                slab,
                pairs,
                pl.BlockSpec((blocks, 1, length, length), lambda r, s: (0, r, 0, 0)),
                pl.BlockSpec((1, heads, length), lambda r, s: (r, 0, 0)),
            ],
            out_specs=(slab, pairs),
            scratch_shapes=[
                pltpu.VMEM((blocks, HD, length), BF),
                pltpu.VMEM((blocks, length, HD), F32),
                pltpu.VMEM((blocks, length, HD), F32),
                pltpu.VMEM((GROUP, HD, length), F32),
                pltpu.VMEM((heads, 1, length), F32),
            ],
        ),
        compiler_params=pltpu.CompilerParams(vmem_limit_bytes=40 * 2**20),
        cost_estimate=pl.CostEstimate(
            flops=rows * heads * length * 4 * length * HD * 10,
            bytes_accessed=8 * tokens * width,
            transcendentals=rows * heads * length * 4 * length,
        ),
        name="attention_backward",
    )(span, queries, grad_out, out, keyval, bias, logs)


def swap(x, axis, count, bit):
    return lax.ppermute(x, axis, [(i, i ^ bit) for i in range(count)])


def low_bit(slot):
    return slot & -slot


def high_bit(slot):
    return 1 << (slot.bit_length() - 1)


def by_bits(count):
    return sorted(range(1, count), key=lambda slot: (bin(slot).count("1"), slot))


def gather_slots(x, axis, count):
    half = x.shape[0] // 2
    slots = {0: (x[:half], x[half:], x)}
    for slot in by_bits(count):
        high, low = high_bit(slot), low_bit(slot)
        if high == low:
            whole = swap(x, axis, count, high)
            slots[slot] = (whole[:half], whole[half:], whole)
        else:
            first = swap(slots[slot ^ high][0], axis, count, high)
            second = swap(slots[slot ^ low][1], axis, count, low)
            slots[slot] = (first, second, None)
    return [
        slots[slot][2] if slots[slot][2] is not None else jnp.concatenate(slots[slot][:2])
        for slot in range(count)
    ]


def scatter_slots(blocks, axis, count):
    half = blocks[0].shape[0] // 2
    parts = {slot: [blocks[slot][:half], blocks[slot][half:]] for slot in range(count)}
    whole = dict(enumerate(blocks))

    def add(slot, which, value):
        parts[slot][which] = (
            parts[slot][which].astype(F32) + value.astype(F32)
        ).astype(blocks[slot].dtype)
        whole[slot] = None

    for slot in reversed(by_bits(count)):
        high, low = high_bit(slot), low_bit(slot)
        if high == low:
            value = whole[slot] if whole[slot] is not None else jnp.concatenate(parts[slot])
            got = swap(value, axis, count, high)
            add(0, 0, got[:half])
            add(0, 1, got[half:])
        else:
            add(slot ^ high, 0, swap(parts[slot][0], axis, count, high))
            add(slot ^ low, 1, swap(parts[slot][1], axis, count, low))
    return jnp.concatenate(parts[0])


def by_owner(slots, own, count):
    shape = slots[0].shape
    whole = jnp.zeros((count,) + shape, slots[0].dtype)
    for slot, value in enumerate(slots):
        start = (own ^ slot,) + (0,) * len(shape)
        whole = lax.dynamic_update_slice(whole, value[None], start)
    return whole.reshape((count * shape[0],) + shape[1:])


def total_over(x, axis, count, own):
    size = x.shape[0] // count
    blocks = [lax.dynamic_slice_in_dim(x, (own ^ slot) * size, size, 0) for slot in range(count)]
    return by_owner(gather_slots(scatter_slots(blocks, axis, count), axis, count), own, count)


def solution(mesh):
    ndp, nmp = mesh.shape["dp"], mesh.shape["mp"]

    def gather_mp(x):
        return lax.all_gather(x, "mp", axis=0, tiled=True)

    def scatter_mp(x):
        return lax.psum_scatter(x, "mp", scatter_dimension=0, tiled=True)

    def body(
        block_input, segments, key_keep, ln1_gain, ln1_bias, w_query, b_query, w_keyval,
        b_value, w_out, b_out, ln2_gain, ln2_bias, w_up, b_up, w_down, b_down, cotangent,
    ):
        length, rows, width = block_input.shape
        tokens = length * rows
        hidden = w_up.shape[1]
        unit = hidden // ndp
        dp, mp = lax.axis_index("dp"), lax.axis_index("mp")

        def by_row(x):
            return jnp.swapaxes(x, 0, 1).reshape(tokens, width)

        def by_place(x):
            return jnp.swapaxes(x.reshape(rows, length, width), 0, 1)

        local = by_row(block_input)
        cot = by_row(cotangent)
        local_input = local.astype(F32)

        query_t = gather_mp(w_query.T)
        out_full = gather_mp(w_out)
        up_t = gather_mp(lax.dynamic_slice_in_dim(w_up, dp * unit, unit, 1).T)
        down = gather_mp(lax.dynamic_slice_in_dim(w_down, dp * unit, unit, 0))
        biases = lax.all_gather(
            jnp.concatenate([b_query, lax.dynamic_slice_in_dim(b_up, dp * unit, unit, 0)]),
            "mp", axis=0, tiled=False,
        )
        query_bias = biases[:, : b_query.shape[0]].reshape(-1)
        up_bias = biases[:, b_query.shape[0] :].reshape(-1)

        places = jnp.arange(nmp * length, dtype=jnp.int32)
        own_places = mp * length + jnp.arange(length, dtype=jnp.int32)
        own_segments = lax.dynamic_slice_in_dim(segments, mp * length, length, 1)
        same_place = places[None, :, None] == own_places[None, None, :]
        allowed = (
            (places[None, :, None] <= own_places[None, None, :])
            & (segments[:, :, None] == own_segments[:, None, :])
            & ((key_keep[:, :, None] == 1) | same_place)
        )
        bias = jnp.where(allowed, 0.0, NEG).astype(BF)
        bias = jnp.swapaxes(bias.reshape(rows, nmp, length, length), 0, 1)
        doc_start = jnp.sum((segments < own_segments[:, :1]).astype(jnp.int32), axis=1)
        span = jnp.concatenate([doc_start // length, mp[None].astype(jnp.int32)])

        normed = layer_norm(local_input, ln1_gain, ln1_bias).astype(BF)
        projected = dot(normed, w_keyval)
        keyval_local = jnp.concatenate(
            [projected[:, :HD], projected[:, HD:] + b_value], axis=1
        ).astype(BF)
        keyval = lax.all_gather(
            keyval_local.reshape(rows, length, 2 * HD), "mp", axis=0, tiled=False
        )
        queries = (dot(normed, query_t, ((1,), (1,))) + query_bias).astype(BF)
        attended, logs = attention_forward(span, queries, keyval, bias, rows)
        residual = local_input + dot(attended, out_full) + b_out
        normed_two = layer_norm(residual, ln2_gain, ln2_bias).astype(BF)

        cot_slots = gather_slots(cot, "dp", ndp)
        two_slots = gather_slots(normed_two, "dp", ndp)
        grown, grad_two, acts, pres = [], [], [], []
        for slot in range(ndp):
            pre_act = dot(two_slots[slot], up_t, ((1,), (1,))) + up_bias
            gelu_value, gelu_pull = jax.vjp(
                lambda inner: jax.nn.gelu(inner, approximate=True), pre_act
            )
            grad_act = dot(cot_slots[slot], down, ((1,), (1,)))
            acts.append(gelu_value.astype(BF))
            pres.append(gelu_pull(grad_act)[0].astype(BF))
        for slot in range(ndp):
            kind = F32 if slot == 0 else BF
            grown.append(dot(acts[slot], down).astype(kind))
            grad_two.append(dot(pres[slot], up_t).astype(kind))
        grad_normed_two = scatter_slots(grad_two, "dp", ndp)
        act_full, pre_full = jnp.concatenate(acts), jnp.concatenate(pres)
        cot_full, two_full = jnp.concatenate(cot_slots), jnp.concatenate(two_slots)
        grad_down = dot(act_full, cot_full, ((0,), (0,))).astype(BF)
        grad_up = dot(pre_full, two_full, ((0,), (0,))).astype(BF)
        grad_b_up = jnp.sum(pre_full, axis=0, dtype=F32)
        grown_sum = scatter_slots(grown, "dp", ndp)
        result = (residual + grown_sum + b_down).astype(BF)

        grad_down = by_owner(gather_slots(scatter_mp(grad_down), "dp", ndp), dp, ndp)
        grad_up = by_owner(gather_slots(scatter_mp(grad_up), "dp", ndp), dp, ndp)

        norm_two_value, norm_two_pull = jax.vjp(layer_norm, residual, ln2_gain, ln2_bias)
        grad_resid_part, grad_ln2_gain, grad_ln2_bias = norm_two_pull(grad_normed_two)
        grad_residual = cot.astype(F32) + grad_resid_part
        grad_b_out = jnp.sum(grad_residual, axis=0)
        grad_b_down = jnp.sum(cot, axis=0, dtype=F32)
        grad_mixed = grad_residual.astype(BF)
        grad_attended = dot(grad_mixed, out_full, ((1,), (1,))).astype(BF)
        grad_out = scatter_mp(dot(attended, grad_mixed, ((0,), (0,))).astype(BF))
        grad_out = total_over(grad_out, "dp", ndp, dp)
        grad_queries, grad_keyval = attention_backward(
            span, queries, grad_attended, attended, keyval, bias, logs, rows
        )
        grad_keyval = scatter_mp(grad_keyval).reshape(tokens, 2 * HD)
        grad_b_query = jnp.sum(grad_queries, axis=0, dtype=F32)
        grad_query = scatter_mp(dot(grad_queries, normed, ((0,), (0,))).astype(BF))
        grad_query = total_over(grad_query, "dp", ndp, dp)
        grad_normed = dot(grad_queries, query_t) + dot(grad_keyval, w_keyval, ((1,), (1,)))
        grad_w_keyval = dot(normed, grad_keyval, ((0,), (0,)))
        grad_b_value = jnp.sum(grad_keyval[:, HD:], axis=0, dtype=F32)
        norm_one_value, norm_one_pull = jax.vjp(layer_norm, local_input, ln1_gain, ln1_bias)
        grad_local, grad_ln1_gain, grad_ln1_bias = norm_one_pull(grad_normed)
        grad_input = (grad_residual + grad_local).astype(BF)

        units = jnp.zeros((nmp, ndp, unit), F32)
        units = lax.dynamic_update_slice(units, grad_b_up.reshape(nmp, 1, unit), (0, dp, 0))
        small = [
            grad_ln1_gain, grad_ln1_bias, grad_ln2_gain, grad_ln2_bias,
            grad_b_out, grad_b_down, grad_b_query, units.reshape(-1), grad_b_value,
        ]
        sizes = [value.shape[0] for value in small]
        sums, grad_w_keyval = lax.psum((jnp.concatenate(small), grad_w_keyval), ("dp", "mp"))
        pieces, place = [], 0
        for size in sizes:
            pieces.append(sums[place : place + size])
            place += size

        def own_part(value, size):
            return lax.dynamic_slice_in_dim(value, mp * size, size, 0)

        return (
            by_place(result),
            by_place(grad_input),
            pieces[0],
            pieces[1],
            grad_query.T.astype(F32),
            own_part(pieces[6], b_query.shape[0]),
            grad_w_keyval,
            pieces[8],
            grad_out.astype(F32),
            pieces[4],
            pieces[2],
            pieces[3],
            grad_up.T.astype(F32),
            own_part(pieces[7], hidden),
            grad_down.astype(F32),
            pieces[5],
        )

    return jax.shard_map(
        body,
        mesh=mesh,
        in_specs=(
            P("mp", "dp", None),
            P("dp", None),
            P("dp", None),
            P(),
            P(),
            P(None, "mp"),
            P("mp"),
            P(),
            P(),
            P("mp", None),
            P(),
            P(),
            P(),
            P(None, "mp"),
            P("mp"),
            P("mp", None),
            P(),
            P("mp", "dp", None),
        ),
        out_specs=(
            P("mp", "dp", None),
            P("mp", "dp", None),
            P(),
            P(),
            P(None, "mp"),
            P("mp"),
            P(),
            P(),
            P("mp", None),
            P(),
            P(),
            P(),
            P(None, "mp"),
            P("mp"),
            P("mp", None),
            P(),
        ),
        check_vma=False,
    )
```

time: 2530 us -> 1290 us (0.51)
  waiting for transfers between devices: 1750 us -> 696 us
  matrix products: 423 us -> 260 us
  other arithmetic: 179 us -> 65.4 us
  local copies, waits for them, and re-layouts: 81 us -> 152 us
  starting transfers between devices: 0.46 us -> 48.6 us
  blocking collectives: 50.3 us -> 18.6 us
    reduce_scatter x5, waiting for transfers between devices: 940 us -> 191 us  [scatter_mp(): return lax.psum_scatter(x, 'mp', scatter_dimension=0, tiled=True)]
    all_gather x4 -> x5, waiting for transfers between devices: 555 us -> 234 us  [the longest x4 214 us: gather_mp(): return lax.all_gather(x, 'mp', axis=0, tiled=True)]
    dot_general x43 -> x27, matrix products: 423 us -> 260 us  [dot(): lax.dot_general(left, right, (dims, ((), ())), preferred_element_type=F32)]
    ppermute x0 -> x40, waiting for transfers between devices: none -> 131 us  [swap(): return lax.ppermute(x, axis, [(i, i ^ bit) for i in range(count)])]
    psum x2 -> x1, waiting for transfers between devices: 259 us -> 139 us  [body(): lax.psum((jnp.concatenate(small), grad_w_keyval), ('dp', 'mp'))]
    convert_element_type x14 -> x16, other arithmetic: 83.8 us -> 30.4 us  [the longest x1 7.1 us: body(): grad_down.astype(F32)]
    dynamic_update_slice x4 -> x13, local copies, waits for them, and re-layouts: 5.33 us -> 57.9 us  [the longest x12 57.9 us: by_owner(): whole = lax.dynamic_update_slice(whole, value[None], start)]
    psum x2 -> x0, blocking collectives: 50.3 us -> none  [the longest x1 39.4 us: body(): lax.psum((grad_w_keyval, grad_b_value, grad_ln1_gain, grad_ln1_bias, grad...]
  transfers between devices with their start and end apart: 11 -> 51, of which waited for: 10 -> 26; matrix products, arithmetic and copies ran while one was open for 7% -> 32% of each run, Pallas kernels for 0% -> 1%
where the time goes in v1:
time: 1290 us; the launch traced here: 1280 us
  waiting for transfers between devices  696 us (54%)
  matrix products  260 us (20%)
  local copies, waits for them, and re-layouts  152 us (12%)
  other arithmetic  65.4 us (5%)
  starting transfers between devices  48.6 us (4%)
  Pallas kernels  23.8 us (2%)
  blocking collectives  18.6 us (1%)
  between operations  16 us (1%)
    dot_general x27, matrix products, dot(): lax.dot_general(left, right, (dims, ((), ())), preferred_element_type=F32)  260 us
    all_gather x4, waiting for transfers between devices, gather_mp(): return lax.all_gather(x, 'mp', axis=0, tiled=True)  214 us
    reduce_scatter x5, waiting for transfers between devices, scatter_mp(): return lax.psum_scatter(x, 'mp', scatter_dimension=0, tiled=True)  191 us
    psum x1, waiting for transfers between devices, body(): lax.psum((jnp.concatenate(small), grad_w_keyval), ('dp', 'mp'))  139 us
    ppermute x40, waiting for transfers between devices, swap(): return lax.ppermute(x, axis, [(i, i ^ bit) for i in range(count)])  131 us
    dynamic_update_slice x12, local copies, waits for them, and re-layouts, by_owner(): whole = lax.dynamic_update_slice(whole, value[None], start)  57.9 us
    ppermute x40, starting transfers between devices, swap(): return lax.ppermute(x, axis, [(i, i ^ bit) for i in range(count)])  48.2 us
    unnamed x187, local copies, waits for them, and re-layouts  39.9 us
  transfers between devices with their start and end apart: 51, of which 26 were waited for; matrix products, arithmetic and copies ran while one was open for 32% of the time, Pallas kernels for 1%

profile of v1, /device:TPU:0, one launch (start us, length us, event | category | flops | bytes accessed | tf_op | source)
XLA Modules:
  0.0 1280.2 jit_solution(7052853489404909963)
XLA Ops:
  34.8 18.6 %all-gather.1 = f32[8,1,512]{2,1,0:T(1,128)S(1)} all-gather(f32[1,1,512]{2,1,0:T(1,128)S(1)} %bitcast.258), channel_id=2, replica_groups=mesh['dp'=4,'mp'=8] {'mp'}, dimensions={0}, use_global_device_ids=true | all-gather | bytes 18432 | tf_op jit(solution)/shard_map/all_gather | solution.py:323
  56.3 21.4 %collective-permute-done.8 = bf16[512,2048]{1,0:T(8,128)(2,1)} collective-permute-done((bf16[512,2048]{1,0:T(8,128)(2,1)}, bf16[512,2048]{1,0:T(8,128)(2,1)}, u32[]{:S(2)}, u32[]{:S(2)}) %collective-permute-start.8) | collective-permute-done | bytes 2097184 | tf_op jit(solution)/shard_map/ppermute | solution.py:218
  104.8 19.7 %all-gather.10.cloned.1.call-done.kv_ref = bf16[8,2,256,256]{3,2,1,0:T(8,128)(2,1)} async-done(((bf16[1,2,256,256]{3,2,1,0:T(8,128)(2,1)}), bf16[8,2,256,256]{3,2,1,0:T(8,128)(2,1)}) %all-gather.10.cloned.1.call-update) | async-done | bytes 2097168 | tf_op jit(solution)/shard_map/all_gather | solution.py:349
  127.7 12.0 attention_forward.1
  141.0 66.6 %all-gather.12.cloned.1.call-done = bf16[2048,2048]{1,0:T(8,128)(2,1)} async-done(((bf16[256,2048]{1,0:T(8,128)(2,1)}), bf16[2048,2048]{1,0:T(8,128)(2,1)}) %all-gather.12.cloned.1.call-update) | async-done | bytes 8388624 | tf_op jit(solution)/shard_map/all_gather | solution.py:294
  223.9 66.1 %all-gather.14.cloned.1.call-done = bf16[2048,2048]{0,1:T(8,128)(2,1)} async-done(((bf16[256,2048]{0,1:T(8,128)(2,1)}), bf16[2048,2048]{0,1:T(8,128)(2,1)}) %all-gather.14.cloned.1.call-update) | async-done | bytes 8388624 | tf_op jit(solution)/shard_map/all_gather | solution.py:294
  300.6 71.1 %all-gather.16.cloned.1.call-done = bf16[2048,2048]{1,0:T(8,128)(2,1)} async-done(((bf16[256,2048]{1,0:T(8,128)(2,1)}), bf16[2048,2048]{1,0:T(8,128)(2,1)}) %all-gather.16.cloned.1.call-update) | async-done | bytes 8388624 | tf_op jit(solution)/shard_map/all_gather | solution.py:294
  371.7 12.5 fusion.17
  434.3 12.3 fusion.31
  458.7 14.7 %multiply_convert_fusion.2 = (bf16[512,2048]{1,0:T(8,128)(2,1)}, bf16[512,2048]{1,0:T(8,128)(2,1)S(1)}, bf16[512,2048]{1,0:T(8,128)(2,1)}, bf16[512,2048]{1,0:T(8,128)(2,1)}, f32[512,2048]{1,0:T(8,128)}) fusion(f32[2048]{0:T(1024)S(1)} %bitcast.262, f32[512,2048]{1,0:T(8,128)} %copy-done.71, f32[512,2048]{1,0:T(8,128)} %copy-done.72, ...), kind=kOutput, calls=%fused_computation.101 | convolution fusion | flops 4336910336 | bytes 35659776 | tf_op jit(solution)/shard_map/dot_general | solution.py:28
  473.4 12.7 fusion.24
  523.7 14.4 %collective-permute-done.6 = bf16[256,2048]{1,0:T(8,128)(2,1)S(1)} collective-permute-done((bf16[256,2048]{1,0:T(8,128)(2,1)S(1)}, bf16[256,2048]{1,0:T(8,128)(2,1)S(1)}, u32[]{:S(2)}, u32[]{:S(2)}) %collective-permute-start.6) | collective-permute-done | bytes 1048608 | tf_op jit(solution)/shard_map/ppermute | solution.py:218
  546.7 37.4 %collective-permute-done.15 = bf16[512,2048]{1,0:T(8,128)(2,1)S(1)} collective-permute-done((bf16[512,2048]{1,0:T(8,128)(2,1)S(1)}, bf16[512,2048]{1,0:T(8,128)(2,1)S(1)}, u32[]{:S(2)}, u32[]{:S(2)}) %collective-permute-start.15) | collective-permute-done | bytes 2097184 | tf_op jit(solution)/shard_map/ppermute | solution.py:218
  589.0 38.3 %collective-permute-done.7 = bf16[512,2048]{1,0:T(8,128)(2,1)} collective-permute-done((bf16[512,2048]{1,0:T(8,128)(2,1)S(1)}, bf16[512,2048]{1,0:T(8,128)(2,1)}, u32[]{:S(2)}, u32[]{:S(2)}) %collective-permute-start.7) | collective-permute-done | bytes 2097184 | tf_op jit(solution)/shard_map/ppermute | solution.py:218
  646.7 11.8 attention_backward.1
  662.2 24.1 %convolution_convert_fusion = bf16[2048,2048]{1,0:T(8,128)(2,1)} fusion(bf16[2048,2048]{1,0:T(8,128)(2,1)} %constant_dynamic-update-slice_fusion.1, bf16[512,2048]{1,0:T(8,128)(2,1)} %copy-done.27, bf16[512,2048]{1,0:T(8,128)(2,1)} %copy-done.29, bf16[512,2048]{1,0:T(8,128)(2,1)} %copy-done.25, bf16[512,2048]{1,0:T(8,128)(2,1)} %copy-done.23), kind=kOutput, calls=%fused_computation.11 | convolution fusion | flops 17217617920 | bytes 25165824 | tf_op jit(solution)/shard_map/dot_general | solution.py:28
  714.2 13.2 %reduce-scatter.6.cloned.1.call-done = bf16[1,2,256,256]{3,2,1,0:T(8,128)(2,1)} async-done(((bf16[8,2,256,256]{3,2,1,0:T(8,128)(2,1)}), bf16[1,2,256,256]{3,2,1,0:T(8,128)(2,1)}) %reduce-scatter.6.cloned.1.call-update) | async-done | bytes 262160 | tf_op jit(solution)/shard_map/reduce_scatter | solution.py:297
  738.0 23.8 %fusion.8 = bf16[2048,2048]{1,0:T(8,128)(2,1)} fusion(bf16[2048,2048]{1,0:T(8,128)(2,1)} %copy-done.39, bf16[512,2048]{1,0:T(8,128)(2,1)} %get-tuple-element.112, bf16[512,2048]{1,0:T(8,128)(2,1)} %get-tuple-element.110, bf16[512,2048]{1,0:T(8,128)(2,1)} %copy-done.75, bf16[512,2048]{1,0:T(8,128)(2,1)} %get-tuple-element.113), kind=kOutput, calls=%fused_computation.10 | convolution fusion | flops 17217617920 | bytes 25165824 | tf_op jit(solution)/shard_map/dot_general | solution.py:28
  787.8 11.3 copy_bitcast_fusion
  799.1 19.5 %reduce-scatter.12.cloned.1.call-done = bf16[256,2048]{1,0:T(8,128)(2,1)} async-done(((bf16[2048,2048]{1,0:T(8,128)(2,1)}), bf16[256,2048]{1,0:T(8,128)(2,1)}) %reduce-scatter.12.cloned.1.call-update) | async-done | bytes 1048592 | tf_op jit(solution)/shard_map/reduce_scatter | solution.py:297
  820.1 138.7 %all-reduce.3.cloned.1.call-done = (f32[22656]{0:T(1024)}, f32[2048,256]{1,0:T(8,128)}) async-done(((f32[22656]{0:T(1024)}, f32[2048,256]{1,0:T(8,128)}), (f32[22656]{0:T(1024)}, f32[2048,256]{1,0:T(8,128)})) %all-reduce.3.cloned.1.call-update) | async-done | bytes 2187792 | tf_op jit(solution)/shard_map/psum | solution.py:414
  964.8 84.9 %reduce-scatter.14.cloned.1.call-done = bf16[256,2048]{1,0:T(8,128)(2,1)} async-done(((bf16[2048,2048]{1,0:T(8,128)(2,1)}), bf16[256,2048]{1,0:T(8,128)(2,1)}) %reduce-scatter.14.cloned.1.call-update) | async-done | bytes 1048592 | tf_op jit(solution)/shard_map/reduce_scatter | solution.py:297
  1093.0 41.5 %dynamic_update_slice.63 = bf16[4,256,2048]{1,0,2:T(4,128)(2,1)} dynamic-update-slice(bf16[4,256,2048]{1,0,2:T(4,128)(2,1)} %copy.59, bf16[1,256,2048]{1,0,2:T(2,128)(2,1)S(1)} %copy.60, s32[]{:T(128)S(6)} %select_n.75, s32[]{:T(128)} %constant.27.clone.1, s32[]{:T(128)} %constant.27.clone.1) | dynamic-update-slice | bytes 2097156 | tf_op jit(solution)/shard_map/dynamic_update_slice | solution.py:280
  1157.2 73.0 %reduce-scatter.10.cloned.1.call-done = bf16[256,2048]{1,0:T(8,128)(2,1)} async-done(((bf16[2048,2048]{1,0:T(8,128)(2,1)}), bf16[256,2048]{1,0:T(8,128)(2,1)}) %reduce-scatter.10.cloned.1.call-update) | async-done | bytes 1048592 | tf_op jit(solution)/shard_map/reduce_scatter | solution.py:297
  (429 shorter events, 404.5 us)
Async XLA Ops:
  7.2 87.8 %all-gather.8.cloned.1.call-start = ((), (), s32[]{:S(2)}) async-start(), calls=%async_computation.5 | async-start | bytes 9437184 | tf_op jit(solution)/shard_map/all_gather | solution.py:294
  8.0 116.6 %all-gather.10.cloned.1.call-start = ((), (), s32[]{:S(2)}) async-start(), calls=%async_computation.6 | async-start | bytes 2359296 | tf_op jit(solution)/shard_map/all_gather | solution.py:349
  17.7 189.9 %all-gather.12.cloned.1.call-start = ((), (), s32[]{:S(2)}) async-start(), calls=%async_computation.7 | async-start | bytes 9437184 | tf_op jit(solution)/shard_map/all_gather | solution.py:294
  18.5 271.6 %all-gather.14.cloned.1.call-start = ((), (), s32[]{:S(2)}) async-start(), calls=%async_computation.8 | async-start | bytes 9437184 | tf_op jit(solution)/shard_map/all_gather | solution.py:294
  20.9 350.8 %all-gather.16.cloned.1.call-start = ((), (), s32[]{:S(2)}) async-start(), calls=%async_computation.9 | async-start | bytes 9437184 | tf_op jit(solution)/shard_map/all_gather | solution.py:294
  23.5 703.9 %reduce-scatter.6.cloned.1.call-start = ((), (), s32[]{:S(2)}) async-start(), calls=%async_computation.10 | async-start | bytes 2359296 | tf_op jit(solution)/shard_map/reduce_scatter | solution.py:297
  80.0 354.2 %collective-permute-start.11 = (bf16[256,2048]{1,0:T(8,128)(2,1)}, bf16[256,2048]{1,0:T(8,128)(2,1)}, u32[]{:S(2)}, u32[]{:S(2)}) collective-permute-start(bf16[256,2048]{1,0:T(8,128)(2,1)} %slice.323), channel_id=1, source_target_pairs={{0,8},{8,0},{16,24},{24,16},{1,9},{9,1},{17,25},{25,17},{2,10},{10... | collective-permute-start | bytes 3145736 | tf_op jit(solution)/shard_map/ppermute | solution.py:218
  82.7 351.6 %collective-permute-start.10 = (bf16[256,2048]{1,0:T(8,128)(2,1)}, bf16[256,2048]{1,0:T(8,128)(2,1)}, u32[]{:S(2)}, u32[]{:S(2)}) collective-permute-start(bf16[256,2048]{1,0:T(8,128)(2,1)} %slice.322), channel_id=1, source_target_pairs={{0,16},{8,24},{16,0},{24,8},{1,17},{9,25},{17,1},{25,9},{2,18},{10... | collective-permute-start | bytes 3145736 | tf_op jit(solution)/shard_map/ppermute | solution.py:218
  221.0 171.1 %collective-permute-start.1 = (bf16[512,2048]{1,0:T(8,128)(2,1)}, bf16[512,2048]{1,0:T(8,128)(2,1)}, u32[]{:S(2)}, u32[]{:S(2)}) collective-permute-start(bf16[512,2048]{1,0:T(8,128)(2,1)} %get-tuple-element.65), channel_id=1, source_target_pairs={{0,8},{8,0},{16,24},{24,16},{1,9},{9,1},{17,25},{25,17},{2,10},{10... | collective-permute-start | bytes 6291464 | tf_op jit(solution)/shard_map/ppermute | solution.py:218
  222.5 168.0 %collective-permute-start = (bf16[512,2048]{1,0:T(8,128)(2,1)}, bf16[512,2048]{1,0:T(8,128)(2,1)S(1)}, u32[]{:S(2)}, u32[]{:S(2)}) collective-permute-start(bf16[512,2048]{1,0:T(8,128)(2,1)} %get-tuple-element.65), channel_id=1, source_target_pairs={{0,16},{8,24},{16,0},{24,8},{1,17},{9,25},{17,1},{25,9},{2,18},{10... | collective-permute-start | bytes 6291464 | tf_op jit(solution)/shard_map/ppermute | solution.py:218
  458.2 63.9 %collective-permute-start.12 = (bf16[256,2048]{1,0:T(8,128)(2,1)}, bf16[256,2048]{1,0:T(8,128)(2,1)S(1)}, u32[]{:S(2)}, u32[]{:S(2)}) collective-permute-start(bf16[256,2048]{1,0:T(8,128)(2,1)} %get-tuple-element.79), channel_id=1, source_target_pairs={{0,8},{8,0},{16,24},{24,16},{1,9},{9,1},{17,25},{25,17},{2,10},{10... | collective-permute-start | bytes 3145736 | tf_op jit(solution)/shard_map/ppermute | solution.py:218
  538.8 88.5 %collective-permute-start.7 = (bf16[512,2048]{1,0:T(8,128)(2,1)S(1)}, bf16[512,2048]{1,0:T(8,128)(2,1)}, u32[]{:S(2)}, u32[]{:S(2)}) collective-permute-start(bf16[512,2048]{1,0:T(8,128)(2,1)S(1)} %pad_maximum_fusion.3), channel_id=1, source_target_pairs={{0,8},{8,0},{16,24},{24,16},{1,9},{9,1},{17,25},{25,17},{2,10},{10... | collective-permute-start | bytes 6291464 | tf_op jit(solution)/shard_map/ppermute | solution.py:218
  541.0 86.3 %collective-permute-start.5 = (bf16[512,2048]{1,0:T(8,128)(2,1)S(1)}, bf16[512,2048]{1,0:T(8,128)(2,1)}, u32[]{:S(2)}, u32[]{:S(2)}) collective-permute-start(bf16[512,2048]{1,0:T(8,128)(2,1)S(1)} %pad_maximum_fusion.2), channel_id=1, source_target_pairs={{0,16},{8,24},{16,0},{24,8},{1,17},{9,25},{17,1},{25,9},{2,18},{10... | collective-permute-start | bytes 6291464 | tf_op jit(solution)/shard_map/ppermute | solution.py:218
  659.8 158.8 %reduce-scatter.12.cloned.1.call-start = ((), (), s32[]{:S(2)}) async-start(), calls=%async_computation.13 | async-start | bytes 9437184 | tf_op jit(solution)/shard_map/reduce_scatter | solution.py:297
  686.3 272.4 %all-reduce.3.cloned.1.call-start = ((), (), s32[]{:S(2)}) async-start(), calls=%async_computation.15 | async-start | bytes 4382720 | tf_op jit(solution)/shard_map/psum | solution.py:414
  738.0 311.7 %reduce-scatter.14.cloned.1.call-start = ((), (), s32[]{:S(2)}) async-start(), calls=%async_computation.14 | async-start | bytes 9437184 | tf_op jit(solution)/shard_map/reduce_scatter | solution.py:297
  761.8 391.4 %reduce-scatter.8.cloned.1.call-start = ((), (), s32[]{:S(2)}) async-start(), calls=%async_computation.11 | async-start | bytes 9437184 | tf_op jit(solution)/shard_map/reduce_scatter | solution.py:297
  770.6 459.6 %reduce-scatter.10.cloned.1.call-start = ((), (), s32[]{:S(2)}) async-start(), calls=%async_computation.12 | async-start | bytes 9437184 | tf_op jit(solution)/shard_map/reduce_scatter | solution.py:297
  818.6 241.2 %collective-permute-start.32 = (bf16[256,2048]{1,0:T(8,128)(2,1)}, bf16[256,2048]{1,0:T(8,128)(2,1)S(1)}, u32[]{:S(2)}, u32[]{:S(2)}) collective-permute-start(bf16[256,2048]{1,0:T(8,128)(2,1)} %reduce-scatter.12.cloned.1.call-done), channel_id=1, source_target_pairs={{0,8},{8,0},{16,24},{24,16},{1,9},{9,1},{17,25},{25,17},{2,10},{10... | collective-permute-start | bytes 3145736 | tf_op jit(solution)/shard_map/ppermute | solution.py:218
  963.3 97.5 %collective-permute-start.33 = (bf16[256,2048]{1,0:T(8,128)(2,1)}, bf16[256,2048]{1,0:T(8,128)(2,1)}, u32[]{:S(2)}, u32[]{:S(2)}) collective-permute-start(bf16[256,2048]{1,0:T(8,128)(2,1)} %reduce-scatter.12.cloned.1.call-done), channel_id=1, source_target_pairs={{0,16},{8,24},{16,0},{24,8},{1,17},{9,25},{17,1},{25,9},{2,18},{10... | collective-permute-start | bytes 3145736 | tf_op jit(solution)/shard_map/ppermute | solution.py:218
  1078.0 65.7 %collective-permute-start.39 = (bf16[128,2048]{1,0:T(8,128)(2,1)}, bf16[128,2048]{1,0:T(8,128)(2,1)}, u32[]{:S(2)}, u32[]{:S(2)}) collective-permute-start(bf16[128,2048]{1,0:T(8,128)(2,1)} %slice.357), channel_id=1, source_target_pairs={{0,8},{8,0},{16,24},{24,16},{1,9},{9,1},{17,25},{25,17},{2,10},{10... | collective-permute-start | bytes 1572872 | tf_op jit(solution)/shard_map/ppermute | solution.py:218
  1078.9 64.9 %collective-permute-start.38 = (bf16[128,2048]{1,0:T(8,128)(2,1)}, bf16[128,2048]{1,0:T(8,128)(2,1)}, u32[]{:S(2)}, u32[]{:S(2)}) collective-permute-start(bf16[128,2048]{1,0:T(8,128)(2,1)} %slice.356), channel_id=1, source_target_pairs={{0,16},{8,24},{16,0},{24,8},{1,17},{9,25},{17,1},{25,9},{2,18},{10... | collective-permute-start | bytes 1572872 | tf_op jit(solution)/shard_map/ppermute | solution.py:218
  1154.3 80.0 %collective-permute-start.16 = (bf16[32,2048]{1,0:T(8,128)(2,1)S(1)}, bf16[32,2048]{1,0:T(8,128)(2,1)S(1)}, u32[]{:S(2)}, u32[]{:S(2)}) collective-permute-start(bf16[32,2048]{1,0:T(8,128)(2,1)S(1)} %get-tuple-element.94), channel_id=1, source_target_pairs={{0,8},{8,0},{16,24},{24,16},{1,9},{9,1},{17,25},{25,17},{2,10},{10... | collective-permute-start | bytes 393224 | tf_op jit(solution)/shard_map/ppermute | solution.py:218
  1156.0 78.3 %collective-permute-start.18 = (bf16[32,2048]{1,0:T(8,128)(2,1)S(1)}, bf16[32,2048]{1,0:T(8,128)(2,1)S(1)}, u32[]{:S(2)}, u32[]{:S(2)}) collective-permute-start(bf16[32,2048]{1,0:T(8,128)(2,1)S(1)} %get-tuple-element.96), channel_id=1, source_target_pairs={{0,16},{8,24},{16,0},{24,8},{1,17},{9,25},{17,1},{25,9},{2,18},{10... | collective-permute-start | bytes 393224 | tf_op jit(solution)/shard_map/ppermute | solution.py:218
  (108 other events, 1475.8 us)
Sparse Core Ops, SparseCore 0:
  9.6 85.3 all-gather.7
  97.2 27.3 all-gather.9
  126.1 81.4 all-gather.11
  209.1 80.8 all-gather.13
  291.5 80.2 all-gather.15
  659.9 67.4 reduce-scatter.5
  730.3 88.2 reduce-scatter.11
  824.8 133.8 all-reduce.2
  961.0 88.6 reduce-scatter.13
  1051.8 87.9 reduce-scatter.7
  1142.2 87.9 reduce-scatter.9
